TPU v7x, 32 devices: a whole 2x2x4 slice. The times are simulated.
32 devices in a mesh: dp: 8 (over z, x), seq: 4 (over y, core).
Axes of the slice: x: 2, y: 2, z: 4, core: 2. Of those that a mesh axis runs over, the one named last changes fastest.
Arguments:
- queries: bfloat16 [4096, 2048], P(('dp', 'seq')), may hold values from -6 to 6
- keys: bfloat16 [4096, 2048], P(('dp', 'seq')), may hold values from -6 to 6
- values: bfloat16 [4096, 2048], P(('dp', 'seq')), may hold values from -6 to 6
- q_gain: float32 [2048], replicated, may hold values from 0.25 to 1.75
- k_gain: float32 [2048], replicated, may hold values from 0.25 to 1.75
- out_grad: bfloat16 [4096, 2048], P(('dp', 'seq')), may hold values from -16 to 16
- segments: int32 [8, 512], P('dp'), may hold values from 0 to 3, never falling along the last dimension, each value on 1 to 256 neighbouring positions
- visible: int32 [8, 512], P('dp'), may hold values 0 or 1
Outputs:
- attn_out: bfloat16 [4096, 2048], P(('dp', 'seq'))
- query_grad: bfloat16 [4096, 2048], P(('dp', 'seq'))
- key_grad: bfloat16 [4096, 2048], P(('dp', 'seq'))
- value_grad: bfloat16 [4096, 2048], P(('dp', 'seq'))
- q_gain_grad: float32 [2048], replicated
- k_gain_grad: float32 [2048], replicated
Inputs may be any that keep to these rules, and one draw needn't show every extreme that they name: `segments`: along each packed sequence the clip numbers never fall; each of the 4 clips holds 1 to 256 slots.
All inputs are finite; a program needn't handle non-finite values. No bound on the sum of `visible` on one device may be relied on, other than what follows from the above.
Results may differ from a plain program's by a relative error of at most 0.012.
The roundings to bfloat16 on the way count: a program that leaves them out, or rounds other values in their place, can miss the bound.
Values may be sent and summed in bfloat16 or wider, within the bound.
No kernel may reach another device: no remote copies, remote signals or barrier semaphores. Data moves between devices by JAX's collectives and lax.ppermute only.
A program may use at most 64 MiB of HBM per device.

v0:
```python
import jax
import jax.numpy as jnp
from jax import lax
from jax.sharding import PartitionSpec as P

D_HEAD = 128
epsilon = 1e-06


def normalize(raw_rows, gain_vec):
    raw_f32 = raw_rows.astype(jnp.float32)
    inv_rms = lax.rsqrt(jnp.mean(raw_f32 * raw_f32, axis=-1, keepdims=True) + epsilon)
    return ((raw_f32 * inv_rms * gain_vec).astype(jnp.bfloat16), inv_rms)


def norm_back(raw_rows, inv_rms, gain_vec, grad_norm):
    raw_f32 = raw_rows.astype(jnp.float32)
    grad_f32 = grad_norm.astype(jnp.float32)
    scaled_grad = gain_vec * grad_f32
    mean_term = jnp.mean(scaled_grad * raw_f32, axis=-1, keepdims=True)
    grad_raw = inv_rms * scaled_grad - raw_f32 * inv_rms**3 * mean_term
    return (grad_raw.astype(jnp.bfloat16), jnp.sum(grad_f32 * raw_f32 * inv_rms, axis=0))


def attend(q_norm, k_norm, val_rows, grad_rows, seg_row, vis_row, keep_out):
    seq_rows, feature_count = q_norm.shape
    head_count = feature_count // D_HEAD
    score_scale = D_HEAD ** (-0.5)
    block_rows = 512
    block_count = seq_rows // block_rows
    k_three = k_norm.reshape(seq_rows, head_count, D_HEAD)
    v_three = val_rows.reshape(seq_rows, head_count, D_HEAD)
    positions = jnp.arange(seq_rows, dtype=jnp.int32)
    key_open = vis_row == 1

    def one_block(totals, block_index):
        block_start = block_index * block_rows
        q_block = lax.dynamic_slice_in_dim(q_norm, block_start, block_rows, 0).reshape(
            block_rows, head_count, D_HEAD
        )
        seg_block = lax.dynamic_slice_in_dim(seg_row, block_start, block_rows, 0)
        pos_block = block_start + jnp.arange(block_rows, dtype=jnp.int32)
        allowed = (seg_block[:, None] == seg_row[None, :]) & (
            key_open[None, :] | (pos_block[:, None] == positions[None, :])
        )
        scores = (
            jnp.einsum("shd,thd->hst", q_block, k_three, preferred_element_type=jnp.float32)
            * score_scale
        )
        scores = jnp.where(allowed[None], scores, -1e30)
        row_max = jnp.max(scores, axis=-1, keepdims=True)
        weights = jnp.exp(scores - row_max)
        attn_prob = weights / jnp.sum(weights, axis=-1, keepdims=True)
        prob_half = attn_prob.astype(jnp.bfloat16)
        block_out = jnp.zeros((block_rows, feature_count), jnp.bfloat16)
        if keep_out:
            block_out = (
                jnp.einsum("hst,thd->shd", prob_half, v_three, preferred_element_type=jnp.float32)
                .reshape(block_rows, feature_count)
                .astype(jnp.bfloat16)
            )
        if grad_rows is None:
            return (totals, (block_out, block_out))
        grad_block = lax.dynamic_slice_in_dim(grad_rows, block_start, block_rows, 0).reshape(
            block_rows, head_count, D_HEAD
        )
        dprob = jnp.einsum("shd,thd->hst", grad_block, v_three, preferred_element_type=jnp.float32)
        value_add = jnp.einsum(
            "hst,shd->thd", prob_half, grad_block, preferred_element_type=jnp.float32
        )
        row_dot = jnp.sum(attn_prob * dprob, axis=-1, keepdims=True)
        score_grad = (attn_prob * (dprob - row_dot) * score_scale).astype(jnp.bfloat16)
        q_grad = (
            jnp.einsum("hst,thd->shd", score_grad, k_three, preferred_element_type=jnp.float32)
            .reshape(block_rows, feature_count)
            .astype(jnp.bfloat16)
        )
        key_add = jnp.einsum(
            "hst,shd->thd", score_grad, q_block, preferred_element_type=jnp.float32
        )
        return ((totals[0] + key_add, totals[1] + value_add), (block_out, q_grad))

    empty = jnp.zeros((seq_rows, head_count, D_HEAD), jnp.float32)
    totals, stacked = lax.scan(one_block, (empty, empty), jnp.arange(block_count, dtype=jnp.int32))
    attn_out = stacked[0].reshape(seq_rows, feature_count)
    if grad_rows is None:
        return attn_out
    q_grad = stacked[1].reshape(seq_rows, feature_count)
    k_grad = totals[0].reshape(seq_rows, feature_count).astype(jnp.bfloat16)
    v_grad = totals[1].reshape(seq_rows, feature_count).astype(jnp.bfloat16)
    return (attn_out, q_grad, k_grad, v_grad)


def per_device(queries, keys, values, q_gain, k_gain, out_grad, segments, visible):
    q_norm, q_inv = normalize(queries, q_gain)
    k_norm, k_inv = normalize(keys, k_gain)
    seg_row = segments[0]
    vis_row = visible[0]
    query_heads, key_heads, value_heads = (
        lax.all_to_all(q_norm, "seq", split_axis=1, concat_axis=0, tiled=True),
        lax.all_to_all(k_norm, "seq", split_axis=1, concat_axis=0, tiled=True),
        lax.all_to_all(values, "seq", split_axis=1, concat_axis=0, tiled=True),
    )
    out_part = attend(query_heads, key_heads, value_heads, None, seg_row, vis_row, True)
    attn_out = lax.all_to_all(out_part, "seq", split_axis=0, concat_axis=1, tiled=True)
    grad_heads = lax.all_to_all(out_grad, "seq", split_axis=1, concat_axis=0, tiled=True)
    unused_out, q_part, k_part, v_part = attend(
        query_heads, key_heads, value_heads, grad_heads, seg_row, vis_row, False
    )
    q_grad, k_grad, value_grad = (
        lax.all_to_all(q_part, "seq", split_axis=0, concat_axis=1, tiled=True),
        lax.all_to_all(k_part, "seq", split_axis=0, concat_axis=1, tiled=True),
        lax.all_to_all(v_part, "seq", split_axis=0, concat_axis=1, tiled=True),
    )
    query_grad, q_gain_part = norm_back(queries, q_inv, q_gain, q_grad)
    key_grad, k_gain_part = norm_back(keys, k_inv, k_gain, k_grad)
    q_gain_grad, k_gain_grad = lax.psum((q_gain_part, k_gain_part), ("dp", "seq"))
    return (attn_out, query_grad, key_grad, value_grad, q_gain_grad, k_gain_grad)


def solution(mesh):
    return jax.shard_map(
        per_device,
        mesh=mesh,
        in_specs=(
            P(("dp", "seq"), None),
            P(("dp", "seq"), None),
            P(("dp", "seq"), None),
            P(),
            P(),
            P(("dp", "seq"), None),
            P("dp", None),
            P("dp", None),
        ),
        out_specs=(
            P(("dp", "seq"), None),
            P(("dp", "seq"), None),
            P(("dp", "seq"), None),
            P(("dp", "seq"), None),
            P(),
            P(),
        ),
        check_vma=False,
    )
```

profile of v0, /device:TPU:0, one launch (start us, length us, event | category | flops | bytes accessed | tf_op | source)
XLA Modules:
  0.0 164.4 jit_solution(12461290162924541765)
XLA Ops:
  0.7 1.3 fusion.31
  2.0 1.2 fusion.33
  3.2 0.8 copy.112
  4.1 4.3 %all-to-all-start = ((bf16[128,4,512]{2,0,1:T(8,128)(2,1)}), bf16[128,4,512]{2,0,1:T(8,128)(2,1)S(1)}, u32[]{:S(2)}, u32[]{:S(2)}) async-start(bf16[128,4,512]{2,0,1:T(8,128)(2,1)} %bitcast.48), calls=%async_computation | async-start | bytes 1048576 | tf_op jit(solution)/shard_map/all_to_all | solution.py:100
  8.4 1.3 fusion.40
  9.8 0.8 copy.111
  10.7 6.5 %all-to-all-done = bf16[128,4,512]{2,0,1:T(8,128)(2,1)S(1)} async-done(((bf16[128,4,512]{2,0,1:T(8,128)(2,1)}), bf16[128,4,512]{2,0,1:T(8,128)(2,1)S(1)}, u32[]{:S(2)}, u32[]{:S(2)}) %all-to-all-start) | async-done | bytes 524320 | tf_op jit(solution)/shard_map/all_to_all | solution.py:100
  17.2 3.5 %all-to-all-start.1 = ((bf16[128,4,512]{2,0,1:T(8,128)(2,1)}), bf16[128,4,512]{2,0,1:T(8,128)(2,1)S(1)}, u32[]{:S(2)}, u32[]{:S(2)}) async-start(bf16[128,4,512]{2,0,1:T(8,128)(2,1)} %bitcast.47), calls=%async_computation.1 | async-start | bytes 1048576 | tf_op jit(solution)/shard_map/all_to_all | solution.py:101
  20.7 0.8 copy.110
  21.5 7.9 %all-to-all-done.1 = bf16[128,4,512]{2,0,1:T(8,128)(2,1)S(1)} async-done(((bf16[128,4,512]{2,0,1:T(8,128)(2,1)}), bf16[128,4,512]{2,0,1:T(8,128)(2,1)S(1)}, u32[]{:S(2)}, u32[]{:S(2)}) %all-to-all-start.1) | async-done | bytes 524320 | tf_op jit(solution)/shard_map/all_to_all | solution.py:101
  29.4 3.5 %all-to-all-start.2 = ((bf16[128,4,512]{2,0,1:T(8,128)(2,1)}), bf16[128,4,512]{2,0,1:T(8,128)(2,1)S(1)}, u32[]{:S(2)}, u32[]{:S(2)}) async-start(bf16[128,4,512]{2,0,1:T(8,128)(2,1)} %bitcast.46), calls=%async_computation.2 | async-start | bytes 1048576 | tf_op jit(solution)/shard_map/all_to_all | solution.py:102
  32.9 0.8 copy.109
  33.8 7.9 %all-to-all-done.2 = bf16[128,4,512]{2,0,1:T(8,128)(2,1)S(1)} async-done(((bf16[128,4,512]{2,0,1:T(8,128)(2,1)}), bf16[128,4,512]{2,0,1:T(8,128)(2,1)S(1)}, u32[]{:S(2)}, u32[]{:S(2)}) %all-to-all-start.2) | async-done | bytes 524320 | tf_op jit(solution)/shard_map/all_to_all | solution.py:102
  41.7 3.5 %all-to-all-start.4 = ((bf16[128,4,512]{2,0,1:T(8,128)(2,1)}), bf16[128,4,512]{2,0,1:T(8,128)(2,1)S(1)}, u32[]{:S(2)}, u32[]{:S(2)}) async-start(bf16[128,4,512]{2,0,1:T(8,128)(2,1)} %bitcast.45), calls=%async_computation.4 | async-start | bytes 1048576 | tf_op jit(solution)/shard_map/all_to_all | solution.py:106
  45.2 0.3 fusion.52
  45.6 1.1 copy.79
  46.9 0.3 copy.75
  47.3 6.6 %all-to-all-done.4 = bf16[128,4,512]{2,0,1:T(8,128)(2,1)S(1)} async-done(((bf16[128,4,512]{2,0,1:T(8,128)(2,1)}), bf16[128,4,512]{2,0,1:T(8,128)(2,1)S(1)}, u32[]{:S(2)}, u32[]{:S(2)}) %all-to-all-start.4) | async-done | bytes 524320 | tf_op jit(solution)/shard_map/all_to_all | solution.py:106
  54.1 4.7 %fusion.66 = (f32[4,512]{1,0:T(4,128)S(1)}, f32[4,512,512]{1,2,0:T(8,128)}) fusion(pred[512,512]{0,1:T(8,128)(4,1)S(1)} %fusion.52, bf16[512,4,128]{0,2,1:T(8,128)(2,1)} %copy.79, bf16[512,4,128]{0,2,1:T(8,128)(2,1)S(1)} %copy.75), kind=kOutput, calls=%fused_computation.80 | convolution fusion | flops 272630272 | bytes 5513216 | tf_op jit(solution)/shard_map/while/body/eval_jaxpr/sub | solution.py:52
  58.7 2.9 %fusion.30 = bf16[512,4,128]{2,0,1:T(8,128)(2,1)S(1)} fusion(bf16[512,4,128]{2,1,0:T(4,128)(2,1)S(1)} %reshape.192, f32[4,512,512]{1,2,0:T(8,128)} %get-tuple-element.92, f32[4,512]{1,0:T(4,128)S(1)} %get-tuple-element.91), kind=kOutput, calls=%fused_computation.33 | convolution fusion | flops 270794752 | bytes 5251072 | tf_op jit(solution)/shard_map/while/body/eval_jaxpr/hst,shd->thd/dot_general | solution.py:68
  61.7 0.4 copy.84
  62.1 1.0 convert_element_type.117
  63.1 3.5 %all-to-all-start.7 = ((bf16[4,128,512]{2,1,0:T(8,128)(2,1)}), bf16[4,128,512]{2,1,0:T(8,128)(2,1)S(1)}, u32[]{:S(2)}, u32[]{:S(2)}) async-start(bf16[4,128,512]{2,1,0:T(8,128)(2,1)} %convert_element_type.117), calls=%async_computation.7 | async-start | bytes 1048576 | tf_op jit(solution)/shard_map/all_to_all | solution.py:113
  66.5 3.1 %fusion.29 = bf16[512,4,128]{2,0,1:T(8,128)(2,1)S(1)} fusion(bf16[512,4,128]{2,1,0:T(4,128)(2,1)S(1)} %reshape.191, f32[4,512,512]{1,2,0:T(8,128)} %get-tuple-element.92, f32[4,512]{1,0:T(4,128)S(1)} %get-tuple-element.91), kind=kOutput, calls=%fused_computation.32 | convolution fusion | flops 270794752 | bytes 5251072 | tf_op jit(solution)/shard_map/while/body/eval_jaxpr/hst,thd->shd/dot_general | solution.py:58
  69.6 0.4 copy.70
  70.1 1.0 convert_element_type.99
  71.1 4.3 %all-to-all-done.7 = bf16[4,128,512]{2,1,0:T(8,128)(2,1)S(1)} async-done(((bf16[4,128,512]{2,1,0:T(8,128)(2,1)}), bf16[4,128,512]{2,1,0:T(8,128)(2,1)S(1)}, u32[]{:S(2)}, u32[]{:S(2)}) %all-to-all-start.7) | async-done | bytes 524320 | tf_op jit(solution)/shard_map/all_to_all | solution.py:113
  75.3 3.5 %all-to-all-start.3 = ((bf16[4,128,512]{2,1,0:T(8,128)(2,1)}), bf16[4,128,512]{2,1,0:T(8,128)(2,1)S(1)}, u32[]{:S(2)}, u32[]{:S(2)}) async-start(bf16[4,128,512]{2,1,0:T(8,128)(2,1)} %convert_element_type.99), calls=%async_computation.3 | async-start | bytes 1048576 | tf_op jit(solution)/shard_map/all_to_all | solution.py:105
  78.8 2.7 %fusion.54 = f32[4,512,512]{1,2,0:T(8,128)} fusion(bf16[512,4,128]{2,1,0:T(4,128)(2,1)S(1)} %reshape.192, bf16[512,4,128]{2,1,0:T(4,128)(2,1)S(1)} %reshape.191), kind=kOutput, calls=%fused_computation.62 | convolution fusion | flops 268435456 | bytes 5242880 | tf_op jit(solution)/shard_map/while/body/eval_jaxpr/shd,thd->hst/dot_general | solution.py:67
  81.5 7.6 %fusion.23 = bf16[512,4,128]{0,2,1:T(8,128)(2,1)S(1)} fusion(bf16[512,4,128]{0,2,1:T(8,128)(2,1)} %copy.79, f32[4,512,512]{1,2,0:T(8,128)} %fusion.54, f32[4,512,512]{1,2,0:T(8,128)} %get-tuple-element.92, f32[4,512]{1,0:T(4,128)S(1)} %get-tuple-element.91), kind=kOutput, calls=%fused_computation.30 | convolution fusion | flops 276040192 | bytes 9445376 | tf_op jit(solution)/shard_map/while/body/eval_jaxpr/hst,shd->thd/dot_general | solution.py:78
  89.2 0.9 copy.81
  90.1 3.5 %all-to-all-start.6 = ((bf16[4,128,512]{1,2,0:T(8,128)(2,1)}), bf16[4,128,512]{1,2,0:T(8,128)(2,1)S(1)}, u32[]{:S(2)}, u32[]{:S(2)}) async-start(bf16[4,128,512]{1,2,0:T(8,128)(2,1)} %copy.81), calls=%async_computation.6 | async-start | bytes 1048576 | tf_op jit(solution)/shard_map/all_to_all | solution.py:112
  93.6 8.5 %fusion.26 = bf16[512,4,128]{0,2,1:T(8,128)(2,1)} fusion(bf16[512,4,128]{0,2,1:T(8,128)(2,1)S(1)} %copy.75, f32[4,512,512]{1,2,0:T(8,128)} %fusion.54, f32[4,512,512]{1,2,0:T(8,128)} %get-tuple-element.92, f32[4,512]{1,0:T(4,128)S(1)} %get-tuple-element.91), kind=kOutput, calls=%fused_computation.31 | convolution fusion | flops 276040192 | bytes 9445376 | tf_op jit(solution)/shard_map/while/body/eval_jaxpr/hst,thd->shd/dot_general | solution.py:74
  102.1 1.2 convert_element_type.103
  103.3 0.9 copy.77
  104.2 4.3 %all-to-all-start.5 = ((bf16[4,128,512]{1,2,0:T(8,128)(2,1)}), bf16[4,128,512]{1,2,0:T(8,128)(2,1)}, u32[]{:S(2)}, u32[]{:S(2)}) async-start(bf16[4,128,512]{1,2,0:T(8,128)(2,1)} %copy.77), calls=%async_computation.5 | async-start | bytes 1048576 | tf_op jit(solution)/shard_map/all_to_all | solution.py:111
  108.5 0.3 copy.85
  108.8 1.0 copy.89
  109.8 0.3 copy.71
  110.1 1.0 copy.88
  111.2 0.3 copy.82
  111.5 5.8 %all-to-all-done.5 = bf16[4,128,512]{1,2,0:T(8,128)(2,1)} async-done(((bf16[4,128,512]{1,2,0:T(8,128)(2,1)}), bf16[4,128,512]{1,2,0:T(8,128)(2,1)}, u32[]{:S(2)}, u32[]{:S(2)}) %all-to-all-start.5) | async-done | bytes 524320 | tf_op jit(solution)/shard_map/all_to_all | solution.py:111
  117.3 2.1 %convert_element_type.120 = f32[4,128,512]{1,2,0:T(8,128)} convert(bf16[4,128,512]{1,2,0:T(8,128)(2,1)} %all-to-all-done.5) | non-fusion elementwise | flops 262144 | bytes 1572864 | tf_op jit(solution)/shard_map/convert_element_type | solution.py:18
  119.4 1.6 copy.78
  121.0 0.6 fusion.39
  121.7 40.3 %all-reduce = (f32[2048]{0:T(1024)}, f32[2048]{0:T(1024)}) all-reduce(f32[2048]{0:T(1024)S(1)} %get-tuple-element.71, f32[2048]{0:T(1024)S(1)} %get-tuple-element.94), channel_id=1, replica_groups=mesh['dp'=8,'seq'=4] {'dp','seq'}, use_global_device_ids=true, to_apply=%region_8.9 | all-reduce | flops 4096 | bytes 32768 | tf_op jit(solution)/shard_map/psum | solution.py:117
  162.0 1.2 fusion.36
  163.2 1.2 fusion.45
  (30 shorter events, 1.0 us)
Async XLA Ops:
  0.6 9.0 %copy-start.1 = (bf16[128,2048]{1,0:T(8,128)(2,1)S(1)}, bf16[128,2048]{1,0:T(8,128)(2,1)}, u32[]{:S(2)}) copy-start(bf16[128,2048]{1,0:T(8,128)(2,1)} %param.9) | copy-start | bytes 1572868
  0.6 9.0 %copy-start.5 = (f32[2048]{0:T(1024)S(1)}, f32[2048]{0:T(1024)}, u32[]{:S(2)}) copy-start(f32[2048]{0:T(1024)} %param.12) | copy-start | bytes 24580
  0.7 20.0 %copy-start.2 = (bf16[128,2048]{1,0:T(8,128)(2,1)S(1)}, bf16[128,2048]{1,0:T(8,128)(2,1)}, u32[]{:S(2)}) copy-start(bf16[128,2048]{1,0:T(8,128)(2,1)} %param.10) | copy-start | bytes 1572868
  3.2 29.7 %copy-start.3 = (bf16[128,2048]{1,0:T(8,128)(2,1)S(1)}, bf16[128,2048]{1,0:T(8,128)(2,1)}, u32[]{:S(2)}) copy-start(bf16[128,2048]{1,0:T(8,128)(2,1)} %param.13) | copy-start | bytes 1572868
  4.1 13.1 %all-to-all-start = ((bf16[128,4,512]{2,0,1:T(8,128)(2,1)}), bf16[128,4,512]{2,0,1:T(8,128)(2,1)S(1)}, u32[]{:S(2)}, u32[]{:S(2)}) async-start(bf16[128,4,512]{2,0,1:T(8,128)(2,1)} %bitcast.48), calls=%async_computation | async-start | bytes 1048576 | tf_op jit(solution)/shard_map/all_to_all | solution.py:100
  8.3 36.8 %copy-start.7 = (s32[1,512]{1,0:T(1,128)S(1)}, s32[1,512]{1,0:T(1,128)}, u32[]{:S(2)}) copy-start(s32[1,512]{1,0:T(1,128)} %param.15) | copy-start | bytes 6148
  8.3 36.8 %copy-start.6 = (s32[1,512]{1,0:T(1,128)S(1)}, s32[1,512]{1,0:T(1,128)}, u32[]{:S(2)}) copy-start(s32[1,512]{1,0:T(1,128)} %param.14) | copy-start | bytes 6148
  17.2 12.3 %all-to-all-start.1 = ((bf16[128,4,512]{2,0,1:T(8,128)(2,1)}), bf16[128,4,512]{2,0,1:T(8,128)(2,1)S(1)}, u32[]{:S(2)}, u32[]{:S(2)}) async-start(bf16[128,4,512]{2,0,1:T(8,128)(2,1)} %bitcast.47), calls=%async_computation.1 | async-start | bytes 1048576 | tf_op jit(solution)/shard_map/all_to_all | solution.py:101
  29.4 12.3 %all-to-all-start.2 = ((bf16[128,4,512]{2,0,1:T(8,128)(2,1)}), bf16[128,4,512]{2,0,1:T(8,128)(2,1)S(1)}, u32[]{:S(2)}, u32[]{:S(2)}) async-start(bf16[128,4,512]{2,0,1:T(8,128)(2,1)} %bitcast.46), calls=%async_computation.2 | async-start | bytes 1048576 | tf_op jit(solution)/shard_map/all_to_all | solution.py:102
  41.7 12.3 %all-to-all-start.4 = ((bf16[128,4,512]{2,0,1:T(8,128)(2,1)}), bf16[128,4,512]{2,0,1:T(8,128)(2,1)S(1)}, u32[]{:S(2)}, u32[]{:S(2)}) async-start(bf16[128,4,512]{2,0,1:T(8,128)(2,1)} %bitcast.45), calls=%async_computation.4 | async-start | bytes 1048576 | tf_op jit(solution)/shard_map/all_to_all | solution.py:106
  63.1 12.3 %all-to-all-start.7 = ((bf16[4,128,512]{2,1,0:T(8,128)(2,1)}), bf16[4,128,512]{2,1,0:T(8,128)(2,1)S(1)}, u32[]{:S(2)}, u32[]{:S(2)}) async-start(bf16[4,128,512]{2,1,0:T(8,128)(2,1)} %convert_element_type.117), calls=%async_computation.7 | async-start | bytes 1048576 | tf_op jit(solution)/shard_map/all_to_all | solution.py:113
  75.3 14.8 %all-to-all-start.3 = ((bf16[4,128,512]{2,1,0:T(8,128)(2,1)}), bf16[4,128,512]{2,1,0:T(8,128)(2,1)S(1)}, u32[]{:S(2)}, u32[]{:S(2)}) async-start(bf16[4,128,512]{2,1,0:T(8,128)(2,1)} %convert_element_type.99), calls=%async_computation.3 | async-start | bytes 1048576 | tf_op jit(solution)/shard_map/all_to_all | solution.py:105
  90.1 14.0 %all-to-all-start.6 = ((bf16[4,128,512]{1,2,0:T(8,128)(2,1)}), bf16[4,128,512]{1,2,0:T(8,128)(2,1)S(1)}, u32[]{:S(2)}, u32[]{:S(2)}) async-start(bf16[4,128,512]{1,2,0:T(8,128)(2,1)} %copy.81), calls=%async_computation.6 | async-start | bytes 1048576 | tf_op jit(solution)/shard_map/all_to_all | solution.py:112
  104.2 13.2 %all-to-all-start.5 = ((bf16[4,128,512]{1,2,0:T(8,128)(2,1)}), bf16[4,128,512]{1,2,0:T(8,128)(2,1)}, u32[]{:S(2)}, u32[]{:S(2)}) async-start(bf16[4,128,512]{1,2,0:T(8,128)(2,1)} %copy.77), calls=%async_computation.5 | async-start | bytes 1048576 | tf_op jit(solution)/shard_map/all_to_all | solution.py:111
  110.0 10.9 %copy-start = (bf16[128,2048]{1,0:T(8,128)(2,1)S(1)}, bf16[128,2048]{1,0:T(8,128)(2,1)}, u32[]{:S(2)}) copy-start(bf16[128,2048]{1,0:T(8,128)(2,1)} %param.8) | copy-start | bytes 1572868
  110.1 10.9 %copy-start.4 = (f32[2048]{0:T(1024)S(1)}, f32[2048]{0:T(1024)}, u32[]{:S(2)}) copy-start(f32[2048]{0:T(1024)} %param.11) | copy-start | bytes 24580
where the time goes:
time: 165 us; the launch traced here: 164 us
  blocking collectives  40.3 us (24%)
  waiting for transfers between devices  39.1 us (24%)
  matrix products  29.5 us (18%)
  starting transfers between devices  29.4 us (18%)
  local copies, waits for them, and re-layouts  15.6 us (9%)
  other arithmetic  9.54 us (6%)
    psum x1, blocking collectives, per_device(): lax.psum((q_gain_part, k_gain_part), ('dp', 'seq'))  40.3 us
    dot_general x1, matrix products, one_block(): jnp.einsum('hst,thd->shd', score_grad, k_three, preferred_element_type=jn...  8.53 us
    all_to_all x1, waiting for transfers between devices, per_device(): lax.all_to_all(k_norm, 'seq', split_axis=1, concat_axis=0, tiled=True)  7.93 us
    all_to_all x1, waiting for transfers between devices, per_device(): lax.all_to_all(values, 'seq', split_axis=1, concat_axis=0, tiled=True)  7.93 us
    dot_general x1, matrix products, one_block(): jnp.einsum('hst,shd->thd', score_grad, q_block, preferred_element_type=jn...  7.62 us
    all_to_all x1, waiting for transfers between devices, per_device(): lax.all_to_all(out_grad, 'seq', split_axis=1, concat_axis=0, tiled=True)  6.63 us
    all_to_all x1, waiting for transfers between devices, per_device(): lax.all_to_all(q_norm, 'seq', split_axis=1, concat_axis=0, tiled=True)  6.49 us
    all_to_all x1, waiting for transfers between devices, per_device(): lax.all_to_all(q_part, 'seq', split_axis=0, concat_axis=1, tiled=True)  5.84 us
  transfers between devices with their start and end apart: 8, of which 6 were waited for; matrix products, arithmetic and copies ran while one was open for 22% of the time, Pallas kernels for 0%

commit v1 on v0

--- a/solution.py
+++ b/solution.py
@@ -114,7 +114,7 @@
     )
     query_grad, q_gain_part = norm_back(queries, q_inv, q_gain, q_grad)
     key_grad, k_gain_part = norm_back(keys, k_inv, k_gain, k_grad)
-    q_gain_grad, k_gain_grad = lax.psum((q_gain_part, k_gain_part), ("dp", "seq"))
+    q_gain_grad, k_gain_grad = lax.psum(lax.psum((q_gain_part, k_gain_part), "seq"), "dp")
     return (attn_out, query_grad, key_grad, value_grad, q_gain_grad, k_gain_grad)
 
 

time: 165 us -> 174 us (1.055)
  blocking collectives: 40.3 us -> 48.7 us
    psum x1 -> x2, blocking collectives: 40.3 us -> 48.7 us  [the longest x1 38.6 us: per_device(): lax.psum(lax.psum((q_gain_part, k_gain_part), 'seq'), 'dp')]
  transfers between devices with their start and end apart: 8 -> 8, of which waited for: 6 -> 6; matrix products, arithmetic and copies ran while one was open for 22% -> 20% of each run, Pallas kernels for 0% -> 0%
where the time goes in v1:
time: 174 us; the launch traced here: 173 us
  blocking collectives  48.7 us (28%)
  waiting for transfers between devices  39.1 us (22%)
  matrix products  29.5 us (17%)
  starting transfers between devices  29.4 us (17%)
  local copies, waits for them, and re-layouts  15.6 us (9%)
  other arithmetic  9.53 us (5%)
    psum x1, blocking collectives, per_device(): lax.psum(lax.psum((q_gain_part, k_gain_part), 'seq'), 'dp')  38.6 us
    psum x1, blocking collectives, per_device(): lax.psum((q_gain_part, k_gain_part), 'seq')  10.1 us
    dot_general x1, matrix products, one_block(): jnp.einsum('hst,thd->shd', score_grad, k_three, preferred_element_type=jn...  8.53 us
    all_to_all x1, waiting for transfers between devices, per_device(): lax.all_to_all(k_norm, 'seq', split_axis=1, concat_axis=0, tiled=True)  7.93 us
    all_to_all x1, waiting for transfers between devices, per_device(): lax.all_to_all(values, 'seq', split_axis=1, concat_axis=0, tiled=True)  7.93 us
    dot_general x1, matrix products, one_block(): jnp.einsum('hst,shd->thd', score_grad, q_block, preferred_element_type=jn...  7.62 us
    all_to_all x1, waiting for transfers between devices, per_device(): lax.all_to_all(out_grad, 'seq', split_axis=1, concat_axis=0, tiled=True)  6.63 us
    all_to_all x1, waiting for transfers between devices, per_device(): lax.all_to_all(q_norm, 'seq', split_axis=1, concat_axis=0, tiled=True)  6.49 us
  transfers between devices with their start and end apart: 8, of which 6 were waited for; matrix products, arithmetic and copies ran while one was open for 20% of the time, Pallas kernels for 0%

profile of v1, /device:TPU:0, one launch (start us, length us, event | category | flops | bytes accessed | tf_op | source)
XLA Modules:
  0.0 172.8 jit_solution(4605501888853644709)
XLA Ops:
  0.7 1.3 fusion.31
  2.0 1.2 fusion.33
  3.2 0.8 copy.112
  4.1 4.3 %all-to-all-start = ((bf16[128,4,512]{2,0,1:T(8,128)(2,1)}), bf16[128,4,512]{2,0,1:T(8,128)(2,1)S(1)}, u32[]{:S(2)}, u32[]{:S(2)}) async-start(bf16[128,4,512]{2,0,1:T(8,128)(2,1)} %bitcast.48), calls=%async_computation | async-start | bytes 1048576 | tf_op jit(solution)/shard_map/all_to_all | solution.py:100
  8.4 1.3 fusion.40
  9.8 0.8 copy.111
  10.7 6.5 %all-to-all-done = bf16[128,4,512]{2,0,1:T(8,128)(2,1)S(1)} async-done(((bf16[128,4,512]{2,0,1:T(8,128)(2,1)}), bf16[128,4,512]{2,0,1:T(8,128)(2,1)S(1)}, u32[]{:S(2)}, u32[]{:S(2)}) %all-to-all-start) | async-done | bytes 524320 | tf_op jit(solution)/shard_map/all_to_all | solution.py:100
  17.2 3.5 %all-to-all-start.1 = ((bf16[128,4,512]{2,0,1:T(8,128)(2,1)}), bf16[128,4,512]{2,0,1:T(8,128)(2,1)S(1)}, u32[]{:S(2)}, u32[]{:S(2)}) async-start(bf16[128,4,512]{2,0,1:T(8,128)(2,1)} %bitcast.47), calls=%async_computation.1 | async-start | bytes 1048576 | tf_op jit(solution)/shard_map/all_to_all | solution.py:101
  20.7 0.8 copy.110
  21.5 7.9 %all-to-all-done.1 = bf16[128,4,512]{2,0,1:T(8,128)(2,1)S(1)} async-done(((bf16[128,4,512]{2,0,1:T(8,128)(2,1)}), bf16[128,4,512]{2,0,1:T(8,128)(2,1)S(1)}, u32[]{:S(2)}, u32[]{:S(2)}) %all-to-all-start.1) | async-done | bytes 524320 | tf_op jit(solution)/shard_map/all_to_all | solution.py:101
  29.4 3.5 %all-to-all-start.2 = ((bf16[128,4,512]{2,0,1:T(8,128)(2,1)}), bf16[128,4,512]{2,0,1:T(8,128)(2,1)S(1)}, u32[]{:S(2)}, u32[]{:S(2)}) async-start(bf16[128,4,512]{2,0,1:T(8,128)(2,1)} %bitcast.46), calls=%async_computation.2 | async-start | bytes 1048576 | tf_op jit(solution)/shard_map/all_to_all | solution.py:102
  32.9 0.8 copy.109
  33.8 7.9 %all-to-all-done.2 = bf16[128,4,512]{2,0,1:T(8,128)(2,1)S(1)} async-done(((bf16[128,4,512]{2,0,1:T(8,128)(2,1)}), bf16[128,4,512]{2,0,1:T(8,128)(2,1)S(1)}, u32[]{:S(2)}, u32[]{:S(2)}) %all-to-all-start.2) | async-done | bytes 524320 | tf_op jit(solution)/shard_map/all_to_all | solution.py:102
  41.7 3.5 %all-to-all-start.4 = ((bf16[128,4,512]{2,0,1:T(8,128)(2,1)}), bf16[128,4,512]{2,0,1:T(8,128)(2,1)S(1)}, u32[]{:S(2)}, u32[]{:S(2)}) async-start(bf16[128,4,512]{2,0,1:T(8,128)(2,1)} %bitcast.45), calls=%async_computation.4 | async-start | bytes 1048576 | tf_op jit(solution)/shard_map/all_to_all | solution.py:106
  45.6 1.1 copy.79
  46.9 0.3 copy.75
  47.3 6.6 %all-to-all-done.4 = bf16[128,4,512]{2,0,1:T(8,128)(2,1)S(1)} async-done(((bf16[128,4,512]{2,0,1:T(8,128)(2,1)}), bf16[128,4,512]{2,0,1:T(8,128)(2,1)S(1)}, u32[]{:S(2)}, u32[]{:S(2)}) %all-to-all-start.4) | async-done | bytes 524320 | tf_op jit(solution)/shard_map/all_to_all | solution.py:106
  54.1 4.7 %fusion.66 = (f32[4,512]{1,0:T(4,128)S(1)}, f32[4,512,512]{1,2,0:T(8,128)}) fusion(pred[512,512]{0,1:T(8,128)(4,1)S(1)} %fusion.52, bf16[512,4,128]{0,2,1:T(8,128)(2,1)} %copy.79, bf16[512,4,128]{0,2,1:T(8,128)(2,1)S(1)} %copy.75), kind=kOutput, calls=%fused_computation.80 | convolution fusion | flops 272630272 | bytes 5513216 | tf_op jit(solution)/shard_map/while/body/eval_jaxpr/sub | solution.py:52
  58.7 2.9 %fusion.30 = bf16[512,4,128]{2,0,1:T(8,128)(2,1)S(1)} fusion(bf16[512,4,128]{2,1,0:T(4,128)(2,1)S(1)} %reshape.192, f32[4,512,512]{1,2,0:T(8,128)} %get-tuple-element.94, f32[4,512]{1,0:T(4,128)S(1)} %get-tuple-element.93), kind=kOutput, calls=%fused_computation.33 | convolution fusion | flops 270794752 | bytes 5251072 | tf_op jit(solution)/shard_map/while/body/eval_jaxpr/hst,shd->thd/dot_general | solution.py:68
  61.7 0.4 copy.84
  62.1 1.0 convert_element_type.117
  63.1 3.5 %all-to-all-start.7 = ((bf16[4,128,512]{2,1,0:T(8,128)(2,1)}), bf16[4,128,512]{2,1,0:T(8,128)(2,1)S(1)}, u32[]{:S(2)}, u32[]{:S(2)}) async-start(bf16[4,128,512]{2,1,0:T(8,128)(2,1)} %convert_element_type.117), calls=%async_computation.7 | async-start | bytes 1048576 | tf_op jit(solution)/shard_map/all_to_all | solution.py:113
  66.5 3.1 %fusion.29 = bf16[512,4,128]{2,0,1:T(8,128)(2,1)S(1)} fusion(bf16[512,4,128]{2,1,0:T(4,128)(2,1)S(1)} %reshape.191, f32[4,512,512]{1,2,0:T(8,128)} %get-tuple-element.94, f32[4,512]{1,0:T(4,128)S(1)} %get-tuple-element.93), kind=kOutput, calls=%fused_computation.32 | convolution fusion | flops 270794752 | bytes 5251072 | tf_op jit(solution)/shard_map/while/body/eval_jaxpr/hst,thd->shd/dot_general | solution.py:58
  69.6 0.4 copy.70
  70.1 1.0 convert_element_type.99
  71.1 4.3 %all-to-all-done.7 = bf16[4,128,512]{2,1,0:T(8,128)(2,1)S(1)} async-done(((bf16[4,128,512]{2,1,0:T(8,128)(2,1)}), bf16[4,128,512]{2,1,0:T(8,128)(2,1)S(1)}, u32[]{:S(2)}, u32[]{:S(2)}) %all-to-all-start.7) | async-done | bytes 524320 | tf_op jit(solution)/shard_map/all_to_all | solution.py:113
  75.3 3.5 %all-to-all-start.3 = ((bf16[4,128,512]{2,1,0:T(8,128)(2,1)}), bf16[4,128,512]{2,1,0:T(8,128)(2,1)S(1)}, u32[]{:S(2)}, u32[]{:S(2)}) async-start(bf16[4,128,512]{2,1,0:T(8,128)(2,1)} %convert_element_type.99), calls=%async_computation.3 | async-start | bytes 1048576 | tf_op jit(solution)/shard_map/all_to_all | solution.py:105
  78.8 2.7 %fusion.54 = f32[4,512,512]{1,2,0:T(8,128)} fusion(bf16[512,4,128]{2,1,0:T(4,128)(2,1)S(1)} %reshape.192, bf16[512,4,128]{2,1,0:T(4,128)(2,1)S(1)} %reshape.191), kind=kOutput, calls=%fused_computation.62 | convolution fusion | flops 268435456 | bytes 5242880 | tf_op jit(solution)/shard_map/while/body/eval_jaxpr/shd,thd->hst/dot_general | solution.py:67
  81.5 7.6 %fusion.23 = bf16[512,4,128]{0,2,1:T(8,128)(2,1)S(1)} fusion(bf16[512,4,128]{0,2,1:T(8,128)(2,1)} %copy.79, f32[4,512,512]{1,2,0:T(8,128)} %fusion.54, f32[4,512,512]{1,2,0:T(8,128)} %get-tuple-element.94, f32[4,512]{1,0:T(4,128)S(1)} %get-tuple-element.93), kind=kOutput, calls=%fused_computation.30 | convolution fusion | flops 276040192 | bytes 9445376 | tf_op jit(solution)/shard_map/while/body/eval_jaxpr/hst,shd->thd/dot_general | solution.py:78
  89.2 0.9 copy.81
  90.1 3.5 %all-to-all-start.6 = ((bf16[4,128,512]{1,2,0:T(8,128)(2,1)}), bf16[4,128,512]{1,2,0:T(8,128)(2,1)S(1)}, u32[]{:S(2)}, u32[]{:S(2)}) async-start(bf16[4,128,512]{1,2,0:T(8,128)(2,1)} %copy.81), calls=%async_computation.6 | async-start | bytes 1048576 | tf_op jit(solution)/shard_map/all_to_all | solution.py:112
  93.6 8.5 %fusion.26 = bf16[512,4,128]{0,2,1:T(8,128)(2,1)} fusion(bf16[512,4,128]{0,2,1:T(8,128)(2,1)S(1)} %copy.75, f32[4,512,512]{1,2,0:T(8,128)} %fusion.54, f32[4,512,512]{1,2,0:T(8,128)} %get-tuple-element.94, f32[4,512]{1,0:T(4,128)S(1)} %get-tuple-element.93), kind=kOutput, calls=%fused_computation.31 | convolution fusion | flops 276040192 | bytes 9445376 | tf_op jit(solution)/shard_map/while/body/eval_jaxpr/hst,thd->shd/dot_general | solution.py:74
  102.1 1.2 convert_element_type.103
  103.3 0.9 copy.77
  104.2 4.3 %all-to-all-start.5 = ((bf16[4,128,512]{1,2,0:T(8,128)(2,1)}), bf16[4,128,512]{1,2,0:T(8,128)(2,1)}, u32[]{:S(2)}, u32[]{:S(2)}) async-start(bf16[4,128,512]{1,2,0:T(8,128)(2,1)} %copy.77), calls=%async_computation.5 | async-start | bytes 1048576 | tf_op jit(solution)/shard_map/all_to_all | solution.py:111
  108.5 0.3 copy.85
  108.8 1.0 copy.89
  109.8 0.3 copy.71
  110.1 1.0 copy.88
  111.2 0.3 copy.82
  111.5 5.8 %all-to-all-done.5 = bf16[4,128,512]{1,2,0:T(8,128)(2,1)} async-done(((bf16[4,128,512]{1,2,0:T(8,128)(2,1)}), bf16[4,128,512]{1,2,0:T(8,128)(2,1)}, u32[]{:S(2)}, u32[]{:S(2)}) %all-to-all-start.5) | async-done | bytes 524320 | tf_op jit(solution)/shard_map/all_to_all | solution.py:111
  117.3 2.1 %convert_element_type.120 = f32[4,128,512]{1,2,0:T(8,128)} convert(bf16[4,128,512]{1,2,0:T(8,128)(2,1)} %all-to-all-done.5) | non-fusion elementwise | flops 262144 | bytes 1572864 | tf_op jit(solution)/shard_map/convert_element_type | solution.py:18
  119.4 1.6 copy.78
  121.0 0.6 fusion.39
  121.7 10.1 %all-reduce.1 = (f32[2048]{0:T(1024)S(1)}, f32[2048]{0:T(1024)S(1)}) all-reduce(f32[2048]{0:T(1024)S(1)} %get-tuple-element.71, f32[2048]{0:T(1024)S(1)} %get-tuple-element.96), channel_id=1, replica_groups=mesh['dp'=8,'seq'=4] {'seq'}, use_global_device_ids=true, to_apply=%region_8.9 | all-reduce | flops 4096 | bytes 32768 | tf_op jit(solution)/shard_map/psum | solution.py:117
  131.8 38.6 %all-reduce = (f32[2048]{0:T(1024)}, f32[2048]{0:T(1024)}) all-reduce(f32[2048]{0:T(1024)S(1)} %get-tuple-element.87, f32[2048]{0:T(1024)S(1)} %get-tuple-element.88), channel_id=1, replica_groups=mesh['dp'=8,'seq'=4] {'dp'}, use_global_device_ids=true, to_apply=%region_9.10 | all-reduce | flops 4096 | bytes 32768 | tf_op jit(solution)/shard_map/psum | solution.py:117
  170.4 1.2 fusion.36
  171.6 1.2 fusion.45
  (31 shorter events, 1.2 us)
Async XLA Ops:
  0.6 9.0 %copy-start.1 = (bf16[128,2048]{1,0:T(8,128)(2,1)S(1)}, bf16[128,2048]{1,0:T(8,128)(2,1)}, u32[]{:S(2)}) copy-start(bf16[128,2048]{1,0:T(8,128)(2,1)} %param.9) | copy-start | bytes 1572868
  0.6 9.0 %copy-start.5 = (f32[2048]{0:T(1024)S(1)}, f32[2048]{0:T(1024)}, u32[]{:S(2)}) copy-start(f32[2048]{0:T(1024)} %param.12) | copy-start | bytes 24580
  0.7 20.0 %copy-start.2 = (bf16[128,2048]{1,0:T(8,128)(2,1)S(1)}, bf16[128,2048]{1,0:T(8,128)(2,1)}, u32[]{:S(2)}) copy-start(bf16[128,2048]{1,0:T(8,128)(2,1)} %param.10) | copy-start | bytes 1572868
  3.2 29.7 %copy-start.3 = (bf16[128,2048]{1,0:T(8,128)(2,1)S(1)}, bf16[128,2048]{1,0:T(8,128)(2,1)}, u32[]{:S(2)}) copy-start(bf16[128,2048]{1,0:T(8,128)(2,1)} %param.13) | copy-start | bytes 1572868
  4.1 13.1 %all-to-all-start = ((bf16[128,4,512]{2,0,1:T(8,128)(2,1)}), bf16[128,4,512]{2,0,1:T(8,128)(2,1)S(1)}, u32[]{:S(2)}, u32[]{:S(2)}) async-start(bf16[128,4,512]{2,0,1:T(8,128)(2,1)} %bitcast.48), calls=%async_computation | async-start | bytes 1048576 | tf_op jit(solution)/shard_map/all_to_all | solution.py:100
  8.3 36.8 %copy-start.7 = (s32[1,512]{1,0:T(1,128)S(1)}, s32[1,512]{1,0:T(1,128)}, u32[]{:S(2)}) copy-start(s32[1,512]{1,0:T(1,128)} %param.15) | copy-start | bytes 6148
  8.3 36.8 %copy-start.6 = (s32[1,512]{1,0:T(1,128)S(1)}, s32[1,512]{1,0:T(1,128)}, u32[]{:S(2)}) copy-start(s32[1,512]{1,0:T(1,128)} %param.14) | copy-start | bytes 6148
  17.2 12.3 %all-to-all-start.1 = ((bf16[128,4,512]{2,0,1:T(8,128)(2,1)}), bf16[128,4,512]{2,0,1:T(8,128)(2,1)S(1)}, u32[]{:S(2)}, u32[]{:S(2)}) async-start(bf16[128,4,512]{2,0,1:T(8,128)(2,1)} %bitcast.47), calls=%async_computation.1 | async-start | bytes 1048576 | tf_op jit(solution)/shard_map/all_to_all | solution.py:101
  29.4 12.3 %all-to-all-start.2 = ((bf16[128,4,512]{2,0,1:T(8,128)(2,1)}), bf16[128,4,512]{2,0,1:T(8,128)(2,1)S(1)}, u32[]{:S(2)}, u32[]{:S(2)}) async-start(bf16[128,4,512]{2,0,1:T(8,128)(2,1)} %bitcast.46), calls=%async_computation.2 | async-start | bytes 1048576 | tf_op jit(solution)/shard_map/all_to_all | solution.py:102
  41.7 12.3 %all-to-all-start.4 = ((bf16[128,4,512]{2,0,1:T(8,128)(2,1)}), bf16[128,4,512]{2,0,1:T(8,128)(2,1)S(1)}, u32[]{:S(2)}, u32[]{:S(2)}) async-start(bf16[128,4,512]{2,0,1:T(8,128)(2,1)} %bitcast.45), calls=%async_computation.4 | async-start | bytes 1048576 | tf_op jit(solution)/shard_map/all_to_all | solution.py:106
  63.1 12.3 %all-to-all-start.7 = ((bf16[4,128,512]{2,1,0:T(8,128)(2,1)}), bf16[4,128,512]{2,1,0:T(8,128)(2,1)S(1)}, u32[]{:S(2)}, u32[]{:S(2)}) async-start(bf16[4,128,512]{2,1,0:T(8,128)(2,1)} %convert_element_type.117), calls=%async_computation.7 | async-start | bytes 1048576 | tf_op jit(solution)/shard_map/all_to_all | solution.py:113
  75.3 14.8 %all-to-all-start.3 = ((bf16[4,128,512]{2,1,0:T(8,128)(2,1)}), bf16[4,128,512]{2,1,0:T(8,128)(2,1)S(1)}, u32[]{:S(2)}, u32[]{:S(2)}) async-start(bf16[4,128,512]{2,1,0:T(8,128)(2,1)} %convert_element_type.99), calls=%async_computation.3 | async-start | bytes 1048576 | tf_op jit(solution)/shard_map/all_to_all | solution.py:105
  90.1 14.0 %all-to-all-start.6 = ((bf16[4,128,512]{1,2,0:T(8,128)(2,1)}), bf16[4,128,512]{1,2,0:T(8,128)(2,1)S(1)}, u32[]{:S(2)}, u32[]{:S(2)}) async-start(bf16[4,128,512]{1,2,0:T(8,128)(2,1)} %copy.81), calls=%async_computation.6 | async-start | bytes 1048576 | tf_op jit(solution)/shard_map/all_to_all | solution.py:112
  104.2 13.2 %all-to-all-start.5 = ((bf16[4,128,512]{1,2,0:T(8,128)(2,1)}), bf16[4,128,512]{1,2,0:T(8,128)(2,1)}, u32[]{:S(2)}, u32[]{:S(2)}) async-start(bf16[4,128,512]{1,2,0:T(8,128)(2,1)} %copy.77), calls=%async_computation.5 | async-start | bytes 1048576 | tf_op jit(solution)/shard_map/all_to_all | solution.py:111
  110.0 10.9 %copy-start = (bf16[128,2048]{1,0:T(8,128)(2,1)S(1)}, bf16[128,2048]{1,0:T(8,128)(2,1)}, u32[]{:S(2)}) copy-start(bf16[128,2048]{1,0:T(8,128)(2,1)} %param.8) | copy-start | bytes 1572868
  110.1 10.9 %copy-start.4 = (f32[2048]{0:T(1024)S(1)}, f32[2048]{0:T(1024)}, u32[]{:S(2)}) copy-start(f32[2048]{0:T(1024)} %param.11) | copy-start | bytes 24580
